TPU v7x, 32 devices: a whole 2x2x4 slice. The times are simulated.
32 devices in a mesh: blk: 16 (over z, x, core), dp: 2 (over y).
Axes of the slice: x: 2, y: 2, z: 4, core: 2. Of those that a mesh axis runs over, the one named last changes fastest.
Arguments:
- inputs: bfloat16 [4096, 1024], P(('blk', 'dp')), may hold values from -6 to 6
- cotangent: bfloat16 [4096, 1024], P(('blk', 'dp')), may hold values from -2.5 to 2.5
- task_ids: int32 [4096], P(('blk', 'dp')), may hold values from 0 to 3
- group_counts: int32 [32, 8], P(('blk', 'dp')), may hold values from 1 to 16, as said below
- task_gate: float32 [4, 16], replicated, may hold values from 0.25 to 2
- w_in: bfloat16 [16, 1024, 2048], P('blk'), may hold values from -0.1875 to 0.1875
- w_out: bfloat16 [16, 2048, 1024], P('blk'), may hold values from -0.125 to 0.125
Outputs:
- input_grad: float32 [4096, 1024], P(('blk', 'dp'))
- grad_in: float32 [16, 1024, 2048], P('blk', 'dp')
- grad_out: float32 [16, 2048, 1024], P('blk', 'dp')
Inputs may be any that keep to these rules, and one draw needn't show every extreme that they name: `group_counts`: in every draw one group has all 16 slots live on every device; the others vary from device to device.
All inputs are finite; a program needn't handle non-finite values.
Results may differ from a plain program's by a relative error of at most 0.0042.
Values may be sent and summed in bfloat16 or wider, within the bound.
A program may use at most 128 MiB of HBM per device.

v0:
```python
import functools

import jax
import jax.numpy as jnp
from jax import lax
from jax.experimental import pallas as pl
from jax.experimental.pallas import tpu as pltpu
from jax.sharding import PartitionSpec as P

grad_scale = 0.0625
VMEM_BYTES = 40 * 1024 * 1024
MESH = pl.DeviceIdType.MESH


def exchange_kernel(
    n, peers, groups, cap, width, hidden, tasks,
    counts_hbm, gate_hbm, ids_hbm, x_hbm, cot_hbm, w1_hbm, w2_hbm,
    xh, sc, act, pc, home,
    counts_ref, gate_ref, ids_ref, cots, tag, pay, buf, w1, w2, ret,
    send1, recv1, send2, recv2, send3, recv3, local_sem,
):
    b = lax.axis_index("blk")
    h = lax.axis_index("dp")
    plane = n * cap
    half, quarter = n // 2, n // 4
    width_part = width // peers
    hidden_part = hidden // peers
    tile = 512
    tiles = hidden // tile
    part_tiles = hidden_part // tile
    side, place = b // half, lax.rem(b, half)
    step, spot = place // quarter, lax.rem(place, quarter)

    def near_target(i):
        return side * half + lax.rem(place - i + half, half)

    def far_target(i):
        return (1 - side) * half + lax.rem(i, 2) * quarter + lax.rem(spot - i // 2 + quarter, quarter)

    def far_slot(i):
        return half + lax.rem(step + side + 1, 2) * quarter + i // 2

    def near_source(i):
        return side * half + lax.rem(place + i, half)

    def far_source(i):
        far = i - half
        ring = far // quarter
        return (1 - side) * half + lax.rem(side + ring, 2) * quarter + lax.rem(spot + lax.rem(far, quarter), quarter)

    def slot_rows(i):
        return pl.ds(pl.multiple_of(i * cap, cap), cap)

    barrier = pltpu.get_barrier_semaphore()

    @pl.loop(1, n)
    def _(k):
        pl.semaphore_signal(barrier, inc=1, device_id=(lax.rem(b + k, n), h), device_id_type=MESH)

    for j in range(1, peers):
        @pl.loop(0, half)
        def _(i):
            pl.semaphore_signal(
                barrier, inc=1, device_id=(near_target(i), lax.rem(h + j, peers)), device_id_type=MESH
            )

    loads = [
        pltpu.make_async_copy(source, target, local_sem.at[6 + at])
        for at, (source, target) in enumerate(
            [(counts_hbm, counts_ref), (gate_hbm, gate_ref), (ids_hbm, ids_ref), (cot_hbm, cots)]
            + [(x_hbm, pay.at[pl.ds(r * groups, groups), :, pl.ds(0, width)]) for r in range(n // groups)]
        )
    ]
    for load in loads:
        load.start()
    get_w1 = pltpu.make_async_copy(w1_hbm.at[0], w1, local_sem.at[3])
    get_w2 = pltpu.make_async_copy(w2_hbm.at[0], w2, local_sem.at[4])
    get_w1.start()
    get_w2.start()
    for load in loads[:4]:
        load.wait()
    slots = groups * cap
    lanes = lax.broadcasted_iota(jnp.int32, (slots, slots), 1)
    places = lax.broadcasted_iota(jnp.int32, (slots, slots), 0)
    ids = jnp.broadcast_to(ids_ref[...].astype(jnp.float32), (slots, slots))
    tag[...] = jnp.broadcast_to(
        jnp.sum(jnp.where(lanes == places, ids, 0.0), axis=1, keepdims=True), tag.shape
    )
    order = lax.broadcasted_iota(jnp.int32, (cap, 1), 0)

    @pl.loop(0, groups)
    def _(g):
        known = tag[slot_rows(g), :][:, 0:1]
        live = order < counts_ref[0, g]
        cot_rows = cots[g].astype(jnp.float32)
        for r in range(n // groups):
            gate = jnp.zeros((cap, 1), jnp.float32)
            for t in range(tasks):
                gate = jnp.where(known == float(t), gate_ref[t, r * groups + g], gate)
            gate = jnp.where(live, gate, 0.0)
            pay[r * groups + g, :, pl.ds(width, width)] = (gate * cot_rows).astype(jnp.bfloat16)

    for load in loads[4:]:
        load.wait()
    own = pltpu.make_async_copy(pay.at[b], buf.at[0, pl.ds(0, cap)], local_sem.at[2])
    own.start()
    pl.semaphore_wait(barrier, n - 1 + (peers - 1) * half)

    def block_out(target, at, slot):
        return pltpu.make_async_remote_copy(
            src_ref=pay.at[target], dst_ref=buf.at[0, slot_rows(slot)],
            send_sem=send1.at[at], recv_sem=recv1.at[slot],
            device_id=(target, h), device_id_type=MESH,
        )

    def across(i, j):
        target = near_target(i)
        return pltpu.make_async_remote_copy(
            src_ref=pay.at[target], dst_ref=buf.at[j, slot_rows(i)],
            send_sem=send2.at[j - 1, i], recv_sem=recv2.at[j - 1, i],
            device_id=(target, lax.rem(h + j, peers)), device_id_type=MESH,
        )

    def forward(i, j):
        return pltpu.make_async_remote_copy(
            src_ref=buf.at[0, slot_rows(i)], dst_ref=buf.at[j, slot_rows(i)],
            send_sem=send2.at[j - 1, i], recv_sem=recv2.at[j - 1, i],
            device_id=(b, lax.rem(h + j, peers)), device_id_type=MESH,
        )

    def homeward(i, target):
        return pltpu.make_async_remote_copy(
            src_ref=ret.at[slot_rows(i)], dst_ref=home.at[b],
            send_sem=send3.at[i], recv_sem=recv3.at[b],
            device_id=(target, h), device_id_type=MESH,
        )

    def home_from(source):
        return pltpu.make_async_remote_copy(
            src_ref=ret.at[slot_rows(0)], dst_ref=home.at[source],
            send_sem=send3.at[0], recv_sem=recv3.at[source],
            device_id=(source, h), device_id_type=MESH,
        )

    for j in range(1, peers):
        across(0, j).start()

    @pl.loop(1, half)
    def _(i):
        block_out(near_target(i), i, i).start()
        for j in range(1, peers):
            across(i, j).start()

    @pl.loop(0, half)
    def _(i):
        block_out(far_target(i), half + i, far_slot(i)).start()

    def pass_on(i):
        block_out(near_target(0), i, i).wait_recv()
        for j in range(1, peers):
            forward(i, j).start()

    early = half + quarter

    @pl.loop(half, early)
    def _(i):
        pass_on(i)

    @pl.loop(1, half)
    def _(i):
        block_out(near_target(0), i, i).wait_recv()

    own.wait()
    get_w1.wait()
    get_w2.wait()

    def rows_forward(j, slot, count, hook):
        first, total = slot * cap, count * cap
        rows = pl.ds(first, total)
        flat = pl.ds(j * plane + first, total)
        sc[flat, :] = buf[j, rows, pl.ds(width, width)]
        xh[flat, :] = buf[j, rows, pl.ds(pl.multiple_of(h * width_part, width_part), width_part)]

        def hidden_tile(q, keep):
            at = lax.rem(h * hidden_part + q * tile, hidden)
            columns = pl.ds(pl.multiple_of(at, tile), tile)
            pre = jnp.dot(
                buf[j, rows, pl.ds(0, width)], w1[:, columns], preferred_element_type=jnp.float32
            )
            sig = jax.nn.sigmoid(pre)
            if keep:
                act[flat, pl.ds(pl.multiple_of(q * tile, tile), tile)] = (pre * sig).astype(jnp.bfloat16)
            cot = lax.dot_general(
                buf[j, rows, pl.ds(width, width)], w2[columns, :], (((1,), (1,)), ((), ())), preferred_element_type=jnp.float32
            )
            pc[flat, columns] = (cot * (sig * (1.0 + pre * (1.0 - sig)))).astype(jnp.bfloat16)
            hook(q)

        @pl.loop(0, part_tiles)
        def _(q):
            hidden_tile(q, True)

        @pl.loop(part_tiles, tiles)
        def _(q):
            hidden_tile(q, False)

    def rows_home(slot, count):
        rows = pl.ds(slot * cap, count * cap)

        @pl.loop(0, width // tile)
        def _(d):
            columns = pl.ds(pl.multiple_of(d * tile, tile), tile)
            grad = lax.dot_general(
                pc[rows, :], w1[columns, :], (((1,), (1,)), ((), ())), preferred_element_type=jnp.float32
            )
            ret[rows, columns] = grad.astype(jnp.bfloat16)

    def partner_rows(j, first, count, hook):
        @pl.loop(first, first + count)
        def _(i):
            forward(i, j).wait_recv()

        rows_forward(j, first, count, hook)

    rows_forward(0, 0, early, lambda q: None)
    rows_home(0, early)
    own_home = pltpu.make_async_copy(ret.at[pl.ds(0, cap)], home.at[b], local_sem.at[5])
    own_home.start()

    @pl.loop(half, early)
    def _(i):
        homeward(i, far_source(i)).start()

    @pl.loop(1, half)
    def _(i):
        homeward(i, near_source(i)).start()

    @pl.loop(early, n)
    def _(i):
        pass_on(i)

    rows_forward(0, early, n - early, lambda q: None)
    rows_home(early, n - early)

    @pl.loop(early, n)
    def _(i):
        homeward(i, far_source(i)).start()

    for j in range(1, peers):
        partner_rows(j, 0, n, lambda q: None)

    own_home.wait()

    @pl.loop(1, n)
    def _(i):
        block_out(near_target(0), i, i).wait_send()
        homeward(i, b).wait_send()

    for j in range(1, peers):
        @pl.loop(0, n)
        def _(i):
            forward(i, j).wait_send()

    @pl.loop(1, n)
    def _(k):
        home_from(lax.rem(b + k, n)).wait_recv()


def on_device(n, peers, inputs, cotangent, task_ids, group_counts, task_gate, w_in, w_out):
    groups = group_counts.shape[1]
    slots, width = inputs.shape
    hidden = w_in.shape[2]
    cap = slots // groups
    tasks = task_gate.shape[0]
    rows = peers * n * cap
    bf16 = jnp.bfloat16
    hbm = pl.BlockSpec(memory_space=pltpu.HBM)
    vmem = pl.BlockSpec(memory_space=pltpu.VMEM)
    dma = pltpu.SemaphoreType.DMA
    xh, sc, act, pc, home = pl.pallas_call(
        functools.partial(exchange_kernel, n, peers, groups, cap, width, hidden, tasks),
        out_shape=(
            pltpu.VMEM((rows, width // peers), bf16),
            pltpu.VMEM((rows, width), bf16),
            pltpu.VMEM((rows, hidden // peers), bf16),
            pltpu.VMEM((rows, hidden), bf16),
            pltpu.VMEM((n, cap, width), bf16),
        ),
        in_specs=[hbm] * 7,
        out_specs=(vmem,) * 5,
        scratch_shapes=[
            pltpu.SMEM(group_counts.shape, jnp.int32),
            pltpu.SMEM(task_gate.shape, jnp.float32),
            pltpu.VMEM((1, slots), jnp.int32),
            pltpu.VMEM((groups, cap, width), bf16),
            pltpu.VMEM((slots, slots), jnp.float32),
            pltpu.VMEM((n, cap, 2 * width), bf16),
            pltpu.VMEM((peers, n * cap, 2 * width), bf16),
            pltpu.VMEM((width, hidden), bf16),
            pltpu.VMEM((hidden, width), bf16),
            pltpu.VMEM((n * cap, width), bf16),
            dma((n,)), dma((n,)), dma((peers - 1, n)), dma((peers - 1, n)), dma((n,)), dma((n,)),
            dma((10 + n // groups,)),
        ],
        compiler_params=pltpu.CompilerParams(
            collective_id=0, has_side_effects=True, vmem_limit_bytes=VMEM_BYTES
        ),
    )(
        *(
            pltpu.with_memory_space_constraint(array, pltpu.HBM)
            for array in (
                group_counts, task_gate, task_ids.reshape(1, slots), inputs.reshape(groups, cap, width),
                cotangent.reshape(groups, cap, width), w_in, w_out,
            )
        )
    )
    turned = (((0,), (0,)), ((), ()))
    first = lax.dot_general(xh, pc, turned, preferred_element_type=jnp.float32) * grad_scale
    second = lax.dot_general(act, sc, turned, preferred_element_type=jnp.float32) * grad_scale
    repeats = n // groups
    input_grad = jnp.sum(home.reshape(repeats, groups * cap, width).astype(jnp.float32), axis=0)
    return input_grad, first[None], second[None]


def solution(mesh):
    in_specs = (
        P(("blk", "dp"), None),
        P(("blk", "dp"), None),
        P(("blk", "dp")),
        P(("blk", "dp"), None),
        P(),
        P("blk", None, None),
        P("blk", None, None),
    )
    out_specs = (P(("blk", "dp"), None), P("blk", "dp", None), P("blk", "dp", None))
    body = functools.partial(on_device, mesh.shape["blk"], mesh.shape["dp"])
    return jax.shard_map(body, mesh=mesh, in_specs=in_specs, out_specs=out_specs, check_vma=False)
```

profile of v0, /device:TPU:0, one launch (start us, length us, event | category | flops | bytes accessed | tf_op | source)
XLA Modules:
  0.0 52.2 jit_solution(6992394394227257479)
XLA Ops:
  0.6 44.1 %shard_map.94 = (bf16[512,512]{1,0:T(8,128)(2,1)S(1)}, bf16[512,1024]{1,0:T(8,128)(2,1)S(1)}, bf16[512,1024]{1,0:T(8,128)(2,1)S(1)}, bf16[512,2048]{1,0:T(8,128)(2,1)S(1)}, bf16[16,16,1024]{2,1,0:T(8,128)(2,1)S(1)}) custom-call(s32[1,8]{1,0:T(1,128)} %counts_hbm.1, f32[4,16]{1,0:T(4,128)} %gate_hbm.1, s32[1,128]{1,0:T(1,128)} %bitcast.18, ...), custom_call_target="tpu_custom_call" | custom-call | tf_op jit(solution)/shard_map/pallas_call | solution.py:280
  44.8 0.9 %convert_reduce_fusion = f32[128,1024]{1,0:T(8,128)} fusion(bf16[2,128,1024]{2,1,0:T(8,128)(2,1)S(1)} %bitcast.15), kind=kLoop, calls=%fused_computation.2 | loop fusion | flops 393216 | bytes 1048576 | tf_op jit(solution)/shard_map/reduce_sum | solution.py:321
  45.7 3.3 %multiply_bitcast_fusion.1 = f32[1,512,2048]{2,1,0:T(8,128)} fusion(bf16[512,512]{1,0:T(8,128)(2,1)S(1)} %get-tuple-element.9, bf16[512,2048]{1,0:T(8,128)(2,1)S(1)} %get-tuple-element.10), kind=kOutput, calls=%fused_computation.1 | convolution fusion | flops 1074790400 | bytes 6815744 | tf_op jit(solution)/shard_map/dot_general | solution.py:318
  48.9 3.3 %multiply_bitcast_fusion = f32[1,1024,1024]{2,1,0:T(8,128)} fusion(bf16[512,1024]{1,0:T(8,128)(2,1)S(1)} %get-tuple-element.11, bf16[512,1024]{1,0:T(8,128)(2,1)S(1)} %get-tuple-element.12), kind=kOutput, calls=%fused_computation | convolution fusion | flops 1074790400 | bytes 6291456 | tf_op jit(solution)/shard_map/dot_general | solution.py:319
where the time goes:
time: 52.4 us; the launch traced here: 52.2 us
  Pallas kernels  44.1 us (84%)
  matrix products  6.59 us (13%)
  other arithmetic  0.88 us (2%)
  between operations  0.64 us (1%)
    pallas_call x1, Pallas kernels, on_device(): pl.pallas_call(functools.partial(exchange_kernel, n, peers, groups, cap,...  44.1 us
    dot_general x1, matrix products, on_device(): lax.dot_general(act, sc, turned, preferred_element_type=jnp.float32)  3.3 us
    dot_general x1, matrix products, on_device(): lax.dot_general(xh, pc, turned, preferred_element_type=jnp.float32)  3.29 us

commit v1 on v0

--- a/solution.py
+++ b/solution.py
@@ -8,21 +8,22 @@
 from jax.sharding import PartitionSpec as P
 
 grad_scale = 0.0625
-VMEM_BYTES = 40 * 1024 * 1024
+VMEM_BYTES = 46 * 1024 * 1024
 MESH = pl.DeviceIdType.MESH
 
 
 def exchange_kernel(
     n, peers, groups, cap, width, hidden, tasks,
     counts_hbm, gate_hbm, ids_hbm, x_hbm, cot_hbm, w1_hbm, w2_hbm,
-    xh, sc, act, pc, home,
-    counts_ref, gate_ref, ids_ref, cots, tag, pay, buf, w1, w2, ret,
+    first, second, home,
+    counts_ref, gate_ref, ids_ref, cots, tag, pay, buf, w1, w2, ret, xh, sc, act, pc,
     send1, recv1, send2, recv2, send3, recv3, local_sem,
 ):
     b = lax.axis_index("blk")
     h = lax.axis_index("dp")
     plane = n * cap
     half, quarter = n // 2, n // 4
+    early = n - quarter
     width_part = width // peers
     hidden_part = hidden // peers
     tile = 512
@@ -31,22 +32,32 @@
     side, place = b // half, lax.rem(b, half)
     step, spot = place // quarter, lax.rem(place, quarter)
 
+    def device_at(z, shift):
+        return z * quarter + lax.rem(spot + shift, quarter)
+
     def near_target(i):
-        return side * half + lax.rem(place - i + half, half)
+        return device_at(2 * side + step, quarter - i)
+
+    def cross_target(i):
+        return device_at(2 * side + 1 - step, quarter - i)
 
     def far_target(i):
-        return (1 - side) * half + lax.rem(i, 2) * quarter + lax.rem(spot - i // 2 + quarter, quarter)
+        return device_at(2 - 2 * side + lax.rem(i, 2), quarter - i // 2)
 
     def far_slot(i):
-        return half + lax.rem(step + side + 1, 2) * quarter + i // 2
+        return (1 + 2 * lax.rem(side + step, 2)) * quarter + i // 2
 
     def near_source(i):
-        return side * half + lax.rem(place + i, half)
-
-    def far_source(i):
-        far = i - half
-        ring = far // quarter
-        return (1 - side) * half + lax.rem(side + ring, 2) * quarter + lax.rem(spot + lax.rem(far, quarter), quarter)
+        return device_at(2 * side + step, i)
+
+    def outer_source(i):
+        return device_at(3 - 3 * side, i)
+
+    def cross_source(i):
+        return device_at(2 * side + 1 - step, i)
+
+    def inner_source(i):
+        return device_at(2 - side, i)
 
     def slot_rows(i):
         return pl.ds(pl.multiple_of(i * cap, cap), cap)
@@ -58,11 +69,7 @@
         pl.semaphore_signal(barrier, inc=1, device_id=(lax.rem(b + k, n), h), device_id_type=MESH)
 
     for j in range(1, peers):
-        @pl.loop(0, half)
-        def _(i):
-            pl.semaphore_signal(
-                barrier, inc=1, device_id=(near_target(i), lax.rem(h + j, peers)), device_id_type=MESH
-            )
+        pl.semaphore_signal(barrier, inc=1, device_id=(b, lax.rem(h + j, peers)), device_id_type=MESH)
 
     loads = [
         pltpu.make_async_copy(source, target, local_sem.at[6 + at])
@@ -104,7 +111,7 @@
         load.wait()
     own = pltpu.make_async_copy(pay.at[b], buf.at[0, pl.ds(0, cap)], local_sem.at[2])
     own.start()
-    pl.semaphore_wait(barrier, n - 1 + (peers - 1) * half)
+    pl.semaphore_wait(barrier, n - 1 + peers - 1)
 
     def block_out(target, at, slot):
         return pltpu.make_async_remote_copy(
@@ -113,14 +120,6 @@
             device_id=(target, h), device_id_type=MESH,
         )
 
-    def across(i, j):
-        target = near_target(i)
-        return pltpu.make_async_remote_copy(
-            src_ref=pay.at[target], dst_ref=buf.at[j, slot_rows(i)],
-            send_sem=send2.at[j - 1, i], recv_sem=recv2.at[j - 1, i],
-            device_id=(target, lax.rem(h + j, peers)), device_id_type=MESH,
-        )
-
     def forward(i, j):
         return pltpu.make_async_remote_copy(
             src_ref=buf.at[0, slot_rows(i)], dst_ref=buf.at[j, slot_rows(i)],
@@ -128,6 +127,13 @@
             device_id=(b, lax.rem(h + j, peers)), device_id_type=MESH,
         )
 
+    def own_across(j):
+        return pltpu.make_async_remote_copy(
+            src_ref=pay.at[b], dst_ref=buf.at[j, slot_rows(0)],
+            send_sem=send2.at[j - 1, 0], recv_sem=recv2.at[j - 1, 0],
+            device_id=(b, lax.rem(h + j, peers)), device_id_type=MESH,
+        )
+
     def homeward(i, target):
         return pltpu.make_async_remote_copy(
             src_ref=ret.at[slot_rows(i)], dst_ref=home.at[b],
@@ -142,42 +148,38 @@
             device_id=(source, h), device_id_type=MESH,
         )
 
-    for j in range(1, peers):
-        across(0, j).start()
-
-    @pl.loop(1, half)
-    def _(i):
-        block_out(near_target(i), i, i).start()
-        for j in range(1, peers):
-            across(i, j).start()
-
-    @pl.loop(0, half)
-    def _(i):
-        block_out(far_target(i), half + i, far_slot(i)).start()
-
     def pass_on(i):
-        block_out(near_target(0), i, i).wait_recv()
+        block_out(b, i, i).wait_recv()
         for j in range(1, peers):
             forward(i, j).start()
 
-    early = half + quarter
-
-    @pl.loop(half, early)
+    @pl.loop(0, half)
+    def _(i):
+        block_out(far_target(i), half + i, far_slot(i)).start()
+
+    @pl.loop(1, quarter)
+    def _(i):
+        block_out(near_target(i), i, i).start()
+
+    @pl.loop(0, quarter)
+    def _(i):
+        block_out(cross_target(i), quarter + i, half + i).start()
+
+    for j in range(1, peers):
+        own_across(j).start()
+
+    @pl.loop(1, half)
     def _(i):
         pass_on(i)
-
-    @pl.loop(1, half)
-    def _(i):
-        block_out(near_target(0), i, i).wait_recv()
 
     own.wait()
     get_w1.wait()
     get_w2.wait()
 
-    def rows_forward(j, slot, count, hook):
-        first, total = slot * cap, count * cap
-        rows = pl.ds(first, total)
-        flat = pl.ds(j * plane + first, total)
+    def rows_forward(j, slot, count):
+        start, total = slot * cap, count * cap
+        rows = pl.ds(start, total)
+        flat = pl.ds((slot // half * peers + j) * half * cap, total)
         sc[flat, :] = buf[j, rows, pl.ds(width, width)]
         xh[flat, :] = buf[j, rows, pl.ds(pl.multiple_of(h * width_part, width_part), width_part)]
 
@@ -194,7 +196,6 @@
                 buf[j, rows, pl.ds(width, width)], w2[columns, :], (((1,), (1,)), ((), ())), preferred_element_type=jnp.float32
             )
             pc[flat, columns] = (cot * (sig * (1.0 + pre * (1.0 - sig)))).astype(jnp.bfloat16)
-            hook(q)
 
         @pl.loop(0, part_tiles)
         def _(q):
@@ -206,55 +207,97 @@
 
     def rows_home(slot, count):
         rows = pl.ds(slot * cap, count * cap)
+        flat = pl.ds(slot * peers * cap, count * cap)
 
         @pl.loop(0, width // tile)
         def _(d):
             columns = pl.ds(pl.multiple_of(d * tile, tile), tile)
             grad = lax.dot_general(
-                pc[rows, :], w1[columns, :], (((1,), (1,)), ((), ())), preferred_element_type=jnp.float32
+                pc[flat, :], w1[columns, :], (((1,), (1,)), ((), ())), preferred_element_type=jnp.float32
             )
             ret[rows, columns] = grad.astype(jnp.bfloat16)
 
-    def partner_rows(j, first, count, hook):
-        @pl.loop(first, first + count)
+    def partner_rows(j, start, count):
+        @pl.loop(start, start + count)
         def _(i):
             forward(i, j).wait_recv()
-
-        rows_forward(j, first, count, hook)
-
-    rows_forward(0, 0, early, lambda q: None)
-    rows_home(0, early)
+        rows_forward(j, start, count)
+
+    turned = (((0,), (0,)), ((), ()))
+    chunk = peers * half * cap
+
+    def grads(part):
+        rows = pl.ds(part * chunk, chunk)
+
+        def add(out, columns, left, right):
+            grad = lax.dot_general(left, right, turned, preferred_element_type=jnp.float32)
+            if part:
+                grad = (out[:, columns] + grad) * grad_scale
+            out[:, columns] = grad
+
+        @pl.loop(0, tiles)
+        def _(q):
+            columns = pl.ds(pl.multiple_of(q * tile, tile), tile)
+            add(first, columns, xh[rows, :], pc[rows, columns])
+
+        @pl.loop(0, width // tile)
+        def _(q):
+            columns = pl.ds(pl.multiple_of(q * tile, tile), tile)
+            add(second, columns, act[rows, :], sc[rows, columns])
+
+    rows_forward(0, 0, half)
+    rows_home(0, half)
     own_home = pltpu.make_async_copy(ret.at[pl.ds(0, cap)], home.at[b], local_sem.at[5])
     own_home.start()
 
+    @pl.loop(1, quarter)
+    def _(i):
+        homeward(i, near_source(i)).start()
+
+    middle = early + quarter // 2
+
+    @pl.loop(half, middle)
+    def _(i):
+        pass_on(i)
+
+    for j in range(1, peers):
+        partner_rows(j, 0, half)
+
+    grads(0)
+
+    @pl.loop(middle, n)
+    def _(i):
+        pass_on(i)
+
+    @pl.loop(quarter, half)
+    def _(i):
+        homeward(i, outer_source(i)).start()
+
+    rows_forward(0, half, half)
+    rows_home(half, half)
+
+    @pl.loop(early, n)
+    def _(i):
+        homeward(i, inner_source(i)).start()
+
     @pl.loop(half, early)
     def _(i):
-        homeward(i, far_source(i)).start()
-
-    @pl.loop(1, half)
-    def _(i):
-        homeward(i, near_source(i)).start()
-
-    @pl.loop(early, n)
-    def _(i):
-        pass_on(i)
-
-    rows_forward(0, early, n - early, lambda q: None)
-    rows_home(early, n - early)
-
-    @pl.loop(early, n)
-    def _(i):
-        homeward(i, far_source(i)).start()
+        homeward(i, cross_source(i)).start()
 
     for j in range(1, peers):
-        partner_rows(j, 0, n, lambda q: None)
+        partner_rows(j, half, half)
+
+    grads(1)
 
     own_home.wait()
 
     @pl.loop(1, n)
     def _(i):
-        block_out(near_target(0), i, i).wait_send()
         homeward(i, b).wait_send()
+
+    @pl.loop(1, n)
+    def _(i):
+        block_out(b, i, i).wait_send()
 
     for j in range(1, peers):
         @pl.loop(0, n)
@@ -264,6 +307,22 @@
     @pl.loop(1, n)
     def _(k):
         home_from(lax.rem(b + k, n)).wait_recv()
+
+
+def finish_kernel(first, second, home, out_rows, out_first, out_second, rows, sem):
+    put_first = pltpu.make_async_copy(first, out_first.at[0], sem.at[0])
+    put_second = pltpu.make_async_copy(second, out_second.at[0], sem.at[1])
+    put_first.start()
+    put_second.start()
+    repeats, total = home.shape[0], jnp.float32(0.0)
+    for r in range(repeats):
+        total = total + home[r].astype(jnp.float32)
+    rows[...] = total
+    put_rows = pltpu.make_async_copy(rows, out_rows, sem.at[2])
+    put_rows.start()
+    put_first.wait()
+    put_second.wait()
+    put_rows.wait()
 
 
 def on_device(n, peers, inputs, cotangent, task_ids, group_counts, task_gate, w_in, w_out):
@@ -277,17 +336,15 @@
     hbm = pl.BlockSpec(memory_space=pltpu.HBM)
     vmem = pl.BlockSpec(memory_space=pltpu.VMEM)
     dma = pltpu.SemaphoreType.DMA
-    xh, sc, act, pc, home = pl.pallas_call(
+    first, second, home = pl.pallas_call(
         functools.partial(exchange_kernel, n, peers, groups, cap, width, hidden, tasks),
         out_shape=(
-            pltpu.VMEM((rows, width // peers), bf16),
-            pltpu.VMEM((rows, width), bf16),
-            pltpu.VMEM((rows, hidden // peers), bf16),
-            pltpu.VMEM((rows, hidden), bf16),
+            pltpu.VMEM((width // peers, hidden), jnp.float32),
+            pltpu.VMEM((hidden // peers, width), jnp.float32),
             pltpu.VMEM((n, cap, width), bf16),
         ),
         in_specs=[hbm] * 7,
-        out_specs=(vmem,) * 5,
+        out_specs=(vmem,) * 3,
         scratch_shapes=[
             pltpu.SMEM(group_counts.shape, jnp.int32),
             pltpu.SMEM(task_gate.shape, jnp.float32),
@@ -299,6 +356,10 @@
             pltpu.VMEM((width, hidden), bf16),
             pltpu.VMEM((hidden, width), bf16),
             pltpu.VMEM((n * cap, width), bf16),
+            pltpu.VMEM((rows, width // peers), bf16),
+            pltpu.VMEM((rows, width), bf16),
+            pltpu.VMEM((rows, hidden // peers), bf16),
+            pltpu.VMEM((rows, hidden), bf16),
             dma((n,)), dma((n,)), dma((peers - 1, n)), dma((peers - 1, n)), dma((n,)), dma((n,)),
             dma((10 + n // groups,)),
         ],
@@ -314,12 +375,18 @@
             )
         )
     )
-    turned = (((0,), (0,)), ((), ()))
-    first = lax.dot_general(xh, pc, turned, preferred_element_type=jnp.float32) * grad_scale
-    second = lax.dot_general(act, sc, turned, preferred_element_type=jnp.float32) * grad_scale
-    repeats = n // groups
-    input_grad = jnp.sum(home.reshape(repeats, groups * cap, width).astype(jnp.float32), axis=0)
-    return input_grad, first[None], second[None]
+    return pl.pallas_call(
+        finish_kernel,
+        out_shape=(
+            jax.ShapeDtypeStruct((slots, width), jnp.float32),
+            jax.ShapeDtypeStruct((1,) + first.shape, jnp.float32),
+            jax.ShapeDtypeStruct((1,) + second.shape, jnp.float32),
+        ),
+        in_specs=[vmem] * 3,
+        out_specs=(hbm,) * 3,
+        scratch_shapes=[pltpu.VMEM((slots, width), jnp.float32), dma((3,))],
+        compiler_params=pltpu.CompilerParams(vmem_limit_bytes=4 * 1024 * 1024),
+    )(first, second, home.reshape(n // groups, slots, width))
 
 
 def solution(mesh):

time: 52.4 us -> 47.1 us (0.90)
  the two profiles are of different devices: /device:TPU:0 before, /device:TPU:9 now
where the time goes in v1:
time: 47.1 us; the launch traced here: 46.1 us
  Pallas kernels  45.5 us (97%)
  between operations  0.64 us (1%)
    pallas_call x1, Pallas kernels, on_device(): pl.pallas_call(functools.partial(exchange_kernel, n, peers, groups, cap,...  42 us
    pallas_call x1, Pallas kernels, on_device(): pl.pallas_call(finish_kernel, out_shape=(jax.ShapeDtypeStruct((slots, wid...  3.46 us

profile of v1, /device:TPU:9, one launch (start us, length us, event | category | flops | bytes accessed | tf_op | source)
XLA Modules:
  0.0 46.1 jit_solution(5332003659770798197)
XLA Ops:
  0.6 42.0 %shard_map.94 = (f32[512,2048]{1,0:T(8,128)S(1)}, f32[1024,1024]{1,0:T(8,128)S(1)}, bf16[16,16,1024]{2,1,0:T(8,128)(2,1)S(1)}) custom-call(s32[1,8]{1,0:T(1,128)} %counts_hbm.1, f32[4,16]{1,0:T(4,128)} %gate_hbm.1, s32[1,128]{1,0:T(1,128)} %bitcast.7, bf16[8,16,1024]{2,1,0:T(8,128)(2,1)} %bitcast.5, bf16[8,16,1024]{2,1,0:T(8,128)(2,1)} %bitcast.6, ...), custom_call_target="tpu_custom_call" | custom-call | tf_op jit(solution)/shard_map/pallas_call | solution.py:339
  42.6 3.5 %shard_map.95 = (f32[128,1024]{1,0:T(8,128)}, f32[1,512,2048]{2,1,0:T(8,128)}, f32[1,1024,1024]{2,1,0:T(8,128)}) custom-call(f32[512,2048]{1,0:T(8,128)S(1)} %get-tuple-element.6.first, f32[1024,1024]{1,0:T(8,128)S(1)} %get-tuple-element.7.second, bf16[2,128,1024]{2,1,0:T(8,128)(2,1)S(1)} %bitcast.4), custom_call_target="tpu_custom_call" | custom-call | tf_op jit(solution)/shard_map/pallas_call | solution.py:378

commit v2 on v1

--- a/solution.py
+++ b/solution.py
@@ -9,6 +9,8 @@
 
 grad_scale = 0.0625
 VMEM_BYTES = 46 * 1024 * 1024
+PIECES = 4
+RELEASE = 1
 MESH = pl.DeviceIdType.MESH
 
 
@@ -69,7 +71,11 @@
         pl.semaphore_signal(barrier, inc=1, device_id=(lax.rem(b + k, n), h), device_id_type=MESH)
 
     for j in range(1, peers):
-        pl.semaphore_signal(barrier, inc=1, device_id=(b, lax.rem(h + j, peers)), device_id_type=MESH)
+        @pl.loop(0, quarter)
+        def _(i):
+            pl.semaphore_signal(
+                barrier, inc=1, device_id=(near_target(i), lax.rem(h + j, peers)), device_id_type=MESH
+            )
 
     loads = [
         pltpu.make_async_copy(source, target, local_sem.at[6 + at])
@@ -111,66 +117,78 @@
         load.wait()
     own = pltpu.make_async_copy(pay.at[b], buf.at[0, pl.ds(0, cap)], local_sem.at[2])
     own.start()
-    pl.semaphore_wait(barrier, n - 1 + peers - 1)
-
-    def block_out(target, at, slot):
+    pl.semaphore_wait(barrier, n - 1 + (peers - 1) * quarter)
+
+    def block_out(target, slot):
         return pltpu.make_async_remote_copy(
             src_ref=pay.at[target], dst_ref=buf.at[0, slot_rows(slot)],
-            send_sem=send1.at[at], recv_sem=recv1.at[slot],
+            send_sem=send1.at[0], recv_sem=recv1.at[slot],
             device_id=(target, h), device_id_type=MESH,
         )
 
     def forward(i, j):
         return pltpu.make_async_remote_copy(
             src_ref=buf.at[0, slot_rows(i)], dst_ref=buf.at[j, slot_rows(i)],
-            send_sem=send2.at[j - 1, i], recv_sem=recv2.at[j - 1, i],
+            send_sem=send2.at[j - 1], recv_sem=recv2.at[j - 1, i // half],
             device_id=(b, lax.rem(h + j, peers)), device_id_type=MESH,
         )
 
-    def own_across(j):
+    def across(i, j):
+        target = near_target(i)
         return pltpu.make_async_remote_copy(
-            src_ref=pay.at[b], dst_ref=buf.at[j, slot_rows(0)],
-            send_sem=send2.at[j - 1, 0], recv_sem=recv2.at[j - 1, 0],
-            device_id=(b, lax.rem(h + j, peers)), device_id_type=MESH,
+            src_ref=pay.at[target], dst_ref=buf.at[j, slot_rows(i)],
+            send_sem=send2.at[j - 1], recv_sem=recv2.at[j - 1, i // half],
+            device_id=(target, lax.rem(h + j, peers)), device_id_type=MESH,
         )
 
     def homeward(i, target):
         return pltpu.make_async_remote_copy(
             src_ref=ret.at[slot_rows(i)], dst_ref=home.at[b],
-            send_sem=send3.at[i], recv_sem=recv3.at[b],
+            send_sem=send3.at[0], recv_sem=recv3.at[0],
             device_id=(target, h), device_id_type=MESH,
         )
 
-    def home_from(source):
-        return pltpu.make_async_remote_copy(
-            src_ref=ret.at[slot_rows(0)], dst_ref=home.at[source],
-            send_sem=send3.at[0], recv_sem=recv3.at[source],
-            device_id=(source, h), device_id_type=MESH,
-        )
-
     def pass_on(i):
-        block_out(b, i, i).wait_recv()
+        block_out(b, i).wait_recv()
         for j in range(1, peers):
             forward(i, j).start()
 
     @pl.loop(0, half)
     def _(i):
-        block_out(far_target(i), half + i, far_slot(i)).start()
+        block_out(far_target(i), far_slot(i)).start()
+
+    for j in range(1, peers):
+        @pl.loop(0, quarter)
+        def _(i):
+            across(i, j).start()
 
     @pl.loop(1, quarter)
     def _(i):
-        block_out(near_target(i), i, i).start()
+        block_out(near_target(i), i).start()
 
     @pl.loop(0, quarter)
     def _(i):
-        block_out(cross_target(i), quarter + i, half + i).start()
-
-    for j in range(1, peers):
-        own_across(j).start()
-
-    @pl.loop(1, half)
+        block_out(cross_target(i), half + i).start()
+
+    def pass_second(before, after):
+        outer = lax.rem(side + step + 1, 2)
+        start = before[0] + outer * (before[1] - before[0])
+        stop = after[0] + outer * (after[1] - after[0])
+
+        @pl.loop(half + start, half + stop)
+        def _(i):
+            pass_on(i)
+
+    @pl.loop(quarter, half)
     def _(i):
         pass_on(i)
+
+    points = [(quarter * inner // 4, quarter * outer // 4) for inner, outer in ((0, 0), (0, 4), (2, 5), (3, 6), (6, 7), (8, 8))]
+    pass_second(*points[0:2])
+
+    @pl.loop(1, quarter)
+    def _(i):
+        block_out(b, i).wait_recv()
 
     own.wait()
     get_w1.wait()
@@ -218,9 +236,8 @@
             ret[rows, columns] = grad.astype(jnp.bfloat16)
 
     def partner_rows(j, start, count):
-        @pl.loop(start, start + count)
-        def _(i):
-            forward(i, j).wait_recv()
+        rows = buf.at[j, pl.ds(start * cap, count * cap)]
+        pltpu.make_async_copy(rows, rows, recv2.at[j - 1, start // half]).wait()
         rows_forward(j, start, count)
 
     turned = (((0,), (0,)), ((), ()))
@@ -245,7 +262,13 @@
             columns = pl.ds(pl.multiple_of(q * tile, tile), tile)
             add(second, columns, act[rows, :], sc[rows, columns])
 
+    def release():
+        @pl.loop(quarter, half)
+        def _(i):
+            homeward(i, outer_source(i)).start()
+
     rows_forward(0, 0, half)
+    pass_second(*points[1:3])
     rows_home(0, half)
     own_home = pltpu.make_async_copy(ret.at[pl.ds(0, cap)], home.at[b], local_sem.at[5])
     own_home.start()
@@ -254,24 +277,21 @@
     def _(i):
         homeward(i, near_source(i)).start()
 
-    middle = early + quarter // 2
-
-    @pl.loop(half, middle)
-    def _(i):
-        pass_on(i)
-
+    pass_second(*points[2:4])
     for j in range(1, peers):
         partner_rows(j, 0, half)
+    pass_second(*points[3:5])
+    @pl.when(lax.rem(side + step + 1, 2) < RELEASE)
+    def _():
+        release()
 
     grads(0)
-
-    @pl.loop(middle, n)
-    def _(i):
-        pass_on(i)
-
-    @pl.loop(quarter, half)
-    def _(i):
-        homeward(i, outer_source(i)).start()
+    pass_second(*points[4:6])
+
+    @pl.when(lax.rem(side + step + 1, 2) >= RELEASE)
+    def _():
+        release()
+
 
     rows_forward(0, half, half)
     rows_home(half, half)
@@ -291,38 +311,33 @@
 
     own_home.wait()
 
-    @pl.loop(1, n)
-    def _(i):
-        homeward(i, b).wait_send()
-
-    @pl.loop(1, n)
-    def _(i):
-        block_out(b, i, i).wait_send()
-
+    sent = pay.at[pl.ds(0, n - 1)]
+    pltpu.make_async_copy(sent, sent, send1.at[0]).wait()
     for j in range(1, peers):
-        @pl.loop(0, n)
-        def _(i):
-            forward(i, j).wait_send()
-
-    @pl.loop(1, n)
-    def _(k):
-        home_from(lax.rem(b + k, n)).wait_recv()
+        pltpu.make_async_copy(buf.at[0], buf.at[0], send2.at[j - 1]).wait()
+    gone = ret.at[pl.ds(0, (n - 1) * cap)]
+    pltpu.make_async_copy(gone, gone, send3.at[0]).wait()
+
+    come = home.at[pl.ds(0, n - 1)]
+    pltpu.make_async_copy(come, come, recv3.at[0]).wait()
 
 
 def finish_kernel(first, second, home, out_rows, out_first, out_second, rows, sem):
-    put_first = pltpu.make_async_copy(first, out_first.at[0], sem.at[0])
-    put_second = pltpu.make_async_copy(second, out_second.at[0], sem.at[1])
-    put_first.start()
-    put_second.start()
+    puts = []
+    for source, target in ((first, out_first), (second, out_second)):
+        step = source.shape[0] // PIECES
+        for piece in range(PIECES):
+            part = pl.ds(piece * step, step)
+            puts.append(pltpu.make_async_copy(source.at[part], target.at[0, part], sem.at[len(puts)]))
+            puts[-1].start()
     repeats, total = home.shape[0], jnp.float32(0.0)
     for r in range(repeats):
         total = total + home[r].astype(jnp.float32)
     rows[...] = total
-    put_rows = pltpu.make_async_copy(rows, out_rows, sem.at[2])
-    put_rows.start()
-    put_first.wait()
-    put_second.wait()
-    put_rows.wait()
+    puts.append(pltpu.make_async_copy(rows, out_rows, sem.at[len(puts)]))
+    puts[-1].start()
+    for put in puts:
+        put.wait()
 
 
 def on_device(n, peers, inputs, cotangent, task_ids, group_counts, task_gate, w_in, w_out):
@@ -360,7 +375,7 @@
             pltpu.VMEM((rows, width), bf16),
             pltpu.VMEM((rows, hidden // peers), bf16),
             pltpu.VMEM((rows, hidden), bf16),
-            dma((n,)), dma((n,)), dma((peers - 1, n)), dma((peers - 1, n)), dma((n,)), dma((n,)),
+            dma((1,)), dma((n,)), dma((peers - 1,)), dma((peers - 1, 2)), dma((1,)), dma((1,)),
             dma((10 + n // groups,)),
         ],
         compiler_params=pltpu.CompilerParams(
@@ -384,7 +399,7 @@
         ),
         in_specs=[vmem] * 3,
         out_specs=(hbm,) * 3,
-        scratch_shapes=[pltpu.VMEM((slots, width), jnp.float32), dma((3,))],
+        scratch_shapes=[pltpu.VMEM((slots, width), jnp.float32), dma((2 * PIECES + 1,))],
         compiler_params=pltpu.CompilerParams(vmem_limit_bytes=4 * 1024 * 1024),
     )(first, second, home.reshape(n // groups, slots, width))
 

time: 47.1 us -> 45.2 us (0.960); the launches traced: 46.1 us -> 45 us
  Pallas kernels: 45.5 us -> 44.4 us
    pallas_call x1, Pallas kernels: 42 us -> 40.9 us  [on_device(): pl.pallas_call(functools.partial(exchange_kernel, n, peers, groups, cap,...]
where the time goes in v2:
time: 45.2 us; the launch traced here: 45 us
  Pallas kernels  44.4 us (98%)
  between operations  0.64 us (1%)
    pallas_call x1, Pallas kernels, on_device(): pl.pallas_call(functools.partial(exchange_kernel, n, peers, groups, cap,...  40.9 us
    pallas_call x1, Pallas kernels, on_device(): pl.pallas_call(finish_kernel, out_shape=(jax.ShapeDtypeStruct((slots, wid...  3.52 us

profile of v2, /device:TPU:9, one launch (start us, length us, event | category | flops | bytes accessed | tf_op | source)
XLA Modules:
  0.0 45.0 jit_solution(9812579637981871631)
XLA Ops:
  0.6 40.9 %shard_map.94 = (f32[512,2048]{1,0:T(8,128)S(1)}, f32[1024,1024]{1,0:T(8,128)S(1)}, bf16[16,16,1024]{2,1,0:T(8,128)(2,1)S(1)}) custom-call(s32[1,8]{1,0:T(1,128)} %counts_hbm.1, f32[4,16]{1,0:T(4,128)} %gate_hbm.1, s32[1,128]{1,0:T(1,128)} %bitcast.7, bf16[8,16,1024]{2,1,0:T(8,128)(2,1)} %bitcast.5, bf16[8,16,1024]{2,1,0:T(8,128)(2,1)} %bitcast.6, ...), custom_call_target="tpu_custom_call" | custom-call | tf_op jit(solution)/shard_map/pallas_call | solution.py:354
  41.5 3.5 %shard_map.95 = (f32[128,1024]{1,0:T(8,128)}, f32[1,512,2048]{2,1,0:T(8,128)}, f32[1,1024,1024]{2,1,0:T(8,128)}) custom-call(f32[512,2048]{1,0:T(8,128)S(1)} %get-tuple-element.6.first, f32[1024,1024]{1,0:T(8,128)S(1)} %get-tuple-element.7.second, bf16[2,128,1024]{2,1,0:T(8,128)(2,1)S(1)} %bitcast.4), custom_call_target="tpu_custom_call" | custom-call | tf_op jit(solution)/shard_map/pallas_call | solution.py:393

commit v3 on v2

--- a/solution.py
+++ b/solution.py
@@ -18,12 +18,11 @@
     n, peers, groups, cap, width, hidden, tasks,
     counts_hbm, gate_hbm, ids_hbm, x_hbm, cot_hbm, w1_hbm, w2_hbm,
     first, second, home,
-    counts_ref, gate_ref, ids_ref, cots, tag, pay, buf, w1, w2, ret, xh, sc, act, pc,
+    counts_ref, gate_ref, ids_ref, cots, tag, pay, buf, w1, w2, ret, act, pc,
     send1, recv1, send2, recv2, send3, recv3, local_sem,
 ):
     b = lax.axis_index("blk")
     h = lax.axis_index("dp")
-    plane = n * cap
     half, quarter = n // 2, n // 4
     early = n - quarter
     width_part = width // peers
@@ -63,6 +62,11 @@
 
     def slot_rows(i):
         return pl.ds(pl.multiple_of(i * cap, cap), cap)
+
+    span = half * cap
+
+    def buf_rows(j, i):
+        return pl.ds(pl.multiple_of((i // half * peers + j) * span + lax.rem(i, half) * cap, cap), cap)
 
     barrier = pltpu.get_barrier_semaphore()
 
@@ -115,20 +119,20 @@
 
     for load in loads[4:]:
         load.wait()
-    own = pltpu.make_async_copy(pay.at[b], buf.at[0, pl.ds(0, cap)], local_sem.at[2])
+    own = pltpu.make_async_copy(pay.at[b], buf.at[pl.ds(0, cap)], local_sem.at[2])
     own.start()
     pl.semaphore_wait(barrier, n - 1 + (peers - 1) * quarter)
 
     def block_out(target, slot):
         return pltpu.make_async_remote_copy(
-            src_ref=pay.at[target], dst_ref=buf.at[0, slot_rows(slot)],
+            src_ref=pay.at[target], dst_ref=buf.at[buf_rows(0, slot)],
             send_sem=send1.at[0], recv_sem=recv1.at[slot],
             device_id=(target, h), device_id_type=MESH,
         )
 
     def forward(i, j):
         return pltpu.make_async_remote_copy(
-            src_ref=buf.at[0, slot_rows(i)], dst_ref=buf.at[j, slot_rows(i)],
+            src_ref=buf.at[buf_rows(0, i)], dst_ref=buf.at[buf_rows(j, i)],
             send_sem=send2.at[j - 1], recv_sem=recv2.at[j - 1, i // half],
             device_id=(b, lax.rem(h + j, peers)), device_id_type=MESH,
         )
@@ -136,7 +140,7 @@
     def across(i, j):
         target = near_target(i)
         return pltpu.make_async_remote_copy(
-            src_ref=pay.at[target], dst_ref=buf.at[j, slot_rows(i)],
+            src_ref=pay.at[target], dst_ref=buf.at[buf_rows(j, i)],
             send_sem=send2.at[j - 1], recv_sem=recv2.at[j - 1, i // half],
             device_id=(target, lax.rem(h + j, peers)), device_id_type=MESH,
         )
@@ -183,8 +187,18 @@
     def _(i):
         pass_on(i)
 
-    points = [(quarter * inner // 4, quarter * outer // 4) for inner, outer in ((0, 0), (0, 4), (2, 5), (3, 6), (6, 7), (8, 8))]
-    pass_second(*points[0:2])
+    points = [
+        (quarter * inner // 4, quarter * outer // 4)
+        for inner, outer in ((0, 0), (0, 4), (1, 5), (2, 5), (2, 6), (3, 6), (6, 6), (7, 7), (8, 8))
+    ]
+    met = []
+
+    def poll(wanted=True):
+        if wanted:
+            met.append(0)
+            pass_second(*points[len(met) - 1:len(met) + 1])
+
+    poll()
 
     @pl.loop(1, quarter)
     def _(i):
@@ -194,56 +208,48 @@
     get_w1.wait()
     get_w2.wait()
 
-    def rows_forward(j, slot, count):
-        start, total = slot * cap, count * cap
+    def rows_forward(start, total, hook=lambda q: None):
         rows = pl.ds(start, total)
-        flat = pl.ds((slot // half * peers + j) * half * cap, total)
-        sc[flat, :] = buf[j, rows, pl.ds(width, width)]
-        xh[flat, :] = buf[j, rows, pl.ds(pl.multiple_of(h * width_part, width_part), width_part)]
-
-        def hidden_tile(q, keep):
+
+        def hidden_tile(q):
             at = lax.rem(h * hidden_part + q * tile, hidden)
             columns = pl.ds(pl.multiple_of(at, tile), tile)
             pre = jnp.dot(
-                buf[j, rows, pl.ds(0, width)], w1[:, columns], preferred_element_type=jnp.float32
+                buf[rows, pl.ds(0, width)], w1[:, columns], preferred_element_type=jnp.float32
             )
             sig = jax.nn.sigmoid(pre)
-            if keep:
-                act[flat, pl.ds(pl.multiple_of(q * tile, tile), tile)] = (pre * sig).astype(jnp.bfloat16)
+            if q < part_tiles:
+                act[rows, pl.ds(q * tile, tile)] = (pre * sig).astype(jnp.bfloat16)
             cot = lax.dot_general(
-                buf[j, rows, pl.ds(width, width)], w2[columns, :], (((1,), (1,)), ((), ())), preferred_element_type=jnp.float32
+                buf[rows, pl.ds(width, width)], w2[columns, :], (((1,), (1,)), ((), ())), preferred_element_type=jnp.float32
             )
-            pc[flat, columns] = (cot * (sig * (1.0 + pre * (1.0 - sig)))).astype(jnp.bfloat16)
-
-        @pl.loop(0, part_tiles)
-        def _(q):
-            hidden_tile(q, True)
-
-        @pl.loop(part_tiles, tiles)
-        def _(q):
-            hidden_tile(q, False)
-
-    def rows_home(slot, count):
-        rows = pl.ds(slot * cap, count * cap)
-        flat = pl.ds(slot * peers * cap, count * cap)
-
-        @pl.loop(0, width // tile)
-        def _(d):
-            columns = pl.ds(pl.multiple_of(d * tile, tile), tile)
+            pc[rows, columns] = (cot * (sig * (1.0 + pre * (1.0 - sig)))).astype(jnp.bfloat16)
+
+        for q in range(tiles):
+            hidden_tile(q)
+            hook(q)
+
+    def rows_home(part, hook=lambda d: None):
+        rows = pl.ds(part * span, span)
+        flat = pl.ds(part * peers * span, span)
+
+        for d in range(width // tile):
+            columns = pl.ds(d * tile, tile)
             grad = lax.dot_general(
                 pc[flat, :], w1[columns, :], (((1,), (1,)), ((), ())), preferred_element_type=jnp.float32
             )
             ret[rows, columns] = grad.astype(jnp.bfloat16)
-
-    def partner_rows(j, start, count):
-        rows = buf.at[j, pl.ds(start * cap, count * cap)]
-        pltpu.make_async_copy(rows, rows, recv2.at[j - 1, start // half]).wait()
-        rows_forward(j, start, count)
+            hook(d)
+
+    def partner_come(part):
+        for j in range(1, peers):
+            rows = buf.at[pl.ds((part * peers + j) * span, span)]
+            pltpu.make_async_copy(rows, rows, recv2.at[j - 1, part]).wait()
 
     turned = (((0,), (0,)), ((), ()))
-    chunk = peers * half * cap
-
-    def grads(part):
+    chunk = peers * span
+
+    def grads(part, hook=lambda: None):
         rows = pl.ds(part * chunk, chunk)
 
         def add(out, columns, left, right):
@@ -252,24 +258,22 @@
                 grad = (out[:, columns] + grad) * grad_scale
             out[:, columns] = grad
 
-        @pl.loop(0, tiles)
-        def _(q):
-            columns = pl.ds(pl.multiple_of(q * tile, tile), tile)
-            add(first, columns, xh[rows, :], pc[rows, columns])
-
-        @pl.loop(0, width // tile)
-        def _(q):
-            columns = pl.ds(pl.multiple_of(q * tile, tile), tile)
-            add(second, columns, act[rows, :], sc[rows, columns])
+        for q in range(tiles):
+            columns = pl.ds(q * tile, tile)
+            add(first, columns, buf[rows, pl.ds(pl.multiple_of(h * width_part, width_part), width_part)], pc[rows, columns])
+        hook()
+        for q in range(width // tile):
+            columns = pl.ds(q * tile, tile)
+            add(second, columns, act[rows, :], buf[rows, pl.ds(width + q * tile, tile)])
 
     def release():
         @pl.loop(quarter, half)
         def _(i):
             homeward(i, outer_source(i)).start()
 
-    rows_forward(0, 0, half)
-    pass_second(*points[1:3])
-    rows_home(0, half)
+    rows_forward(0, span)
+    poll()
+    rows_home(0, lambda d: poll(d == 0))
     own_home = pltpu.make_async_copy(ret.at[pl.ds(0, cap)], home.at[b], local_sem.at[5])
     own_home.start()
 
@@ -277,24 +281,24 @@
     def _(i):
         homeward(i, near_source(i)).start()
 
-    pass_second(*points[2:4])
-    for j in range(1, peers):
-        partner_rows(j, 0, half)
-    pass_second(*points[3:5])
+    poll()
+    partner_come(0)
+    rows_forward(span, chunk - span, lambda q: poll(2 * (q + 1) == tiles))
+    poll()
     @pl.when(lax.rem(side + step + 1, 2) < RELEASE)
     def _():
         release()
 
-    grads(0)
-    pass_second(*points[4:6])
+    grads(0, poll)
+    poll()
 
     @pl.when(lax.rem(side + step + 1, 2) >= RELEASE)
     def _():
         release()
 
 
-    rows_forward(0, half, half)
-    rows_home(half, half)
+    rows_forward(chunk, span)
+    rows_home(1)
 
     @pl.loop(early, n)
     def _(i):
@@ -304,8 +308,8 @@
     def _(i):
         homeward(i, cross_source(i)).start()
 
-    for j in range(1, peers):
-        partner_rows(j, half, half)
+    partner_come(1)
+    rows_forward(chunk + span, chunk - span)
 
     grads(1)
 
@@ -314,7 +318,8 @@
     sent = pay.at[pl.ds(0, n - 1)]
     pltpu.make_async_copy(sent, sent, send1.at[0]).wait()
     for j in range(1, peers):
-        pltpu.make_async_copy(buf.at[0], buf.at[0], send2.at[j - 1]).wait()
+        whole = buf.at[pl.ds(0, 2 * span)]
+        pltpu.make_async_copy(whole, whole, send2.at[j - 1]).wait()
     gone = ret.at[pl.ds(0, (n - 1) * cap)]
     pltpu.make_async_copy(gone, gone, send3.at[0]).wait()
 
@@ -367,12 +372,10 @@
             pltpu.VMEM((groups, cap, width), bf16),
             pltpu.VMEM((slots, slots), jnp.float32),
             pltpu.VMEM((n, cap, 2 * width), bf16),
-            pltpu.VMEM((peers, n * cap, 2 * width), bf16),
+            pltpu.VMEM((rows, 2 * width), bf16),
             pltpu.VMEM((width, hidden), bf16),
             pltpu.VMEM((hidden, width), bf16),
             pltpu.VMEM((n * cap, width), bf16),
-            pltpu.VMEM((rows, width // peers), bf16),
-            pltpu.VMEM((rows, width), bf16),
             pltpu.VMEM((rows, hidden // peers), bf16),
             pltpu.VMEM((rows, hidden), bf16),
             dma((1,)), dma((n,)), dma((peers - 1,)), dma((peers - 1, 2)), dma((1,)), dma((1,)),

time: 45.2 us -> 44.7 us (0.989)
  Pallas kernels: 44.4 us -> 43.9 us
    pallas_call x1, Pallas kernels: 40.9 us -> 40.4 us  [on_device(): pl.pallas_call(functools.partial(exchange_kernel, n, peers, groups, cap,...]
where the time goes in v3:
time: 44.7 us; the launch traced here: 44.5 us
  Pallas kernels  43.9 us (98%)
  between operations  0.64 us (1%)
    pallas_call x1, Pallas kernels, on_device(): pl.pallas_call(functools.partial(exchange_kernel, n, peers, groups, cap,...  40.4 us
    pallas_call x1, Pallas kernels, on_device(): pl.pallas_call(finish_kernel, out_shape=(jax.ShapeDtypeStruct((slots, wid...  3.52 us

profile of v3, /device:TPU:9, one launch (start us, length us, event | category | flops | bytes accessed | tf_op | source)
XLA Modules:
  0.0 44.5 jit_solution(15941692331093225602)
XLA Ops:
  0.6 40.4 %shard_map.94 = (f32[512,2048]{1,0:T(8,128)S(1)}, f32[1024,1024]{1,0:T(8,128)S(1)}, bf16[16,16,1024]{2,1,0:T(8,128)(2,1)S(1)}) custom-call(s32[1,8]{1,0:T(1,128)} %counts_hbm.1, f32[4,16]{1,0:T(4,128)} %gate_hbm.1, s32[1,128]{1,0:T(1,128)} %bitcast.7, bf16[8,16,1024]{2,1,0:T(8,128)(2,1)} %bitcast.5, bf16[8,16,1024]{2,1,0:T(8,128)(2,1)} %bitcast.6, ...), custom_call_target="tpu_custom_call" | custom-call | tf_op jit(solution)/shard_map/pallas_call | solution.py:359
  41.0 3.5 %shard_map.95 = (f32[128,1024]{1,0:T(8,128)}, f32[1,512,2048]{2,1,0:T(8,128)}, f32[1,1024,1024]{2,1,0:T(8,128)}) custom-call(f32[512,2048]{1,0:T(8,128)S(1)} %get-tuple-element.6.first, f32[1024,1024]{1,0:T(8,128)S(1)} %get-tuple-element.7.second, bf16[2,128,1024]{2,1,0:T(8,128)(2,1)S(1)} %bitcast.4), custom_call_target="tpu_custom_call" | custom-call | tf_op jit(solution)/shard_map/pallas_call | solution.py:396

commit v4 on v3

--- a/solution.py
+++ b/solution.py
@@ -8,9 +8,20 @@
 from jax.sharding import PartitionSpec as P
 
 grad_scale = 0.0625
-VMEM_BYTES = 46 * 1024 * 1024
+VMEM_BYTES = 51 * 1024 * 1024
 PIECES = 4
-RELEASE = 1
+RELEASE = (2, 2, 2, 1)
+tile = 512
+SCHEDULE = (
+    (((0, 4), (0, 0), (0, 0), (0, 4)),),
+    (((0, 0), (0, 1), (0, 0), (0, 0)),),
+    (((0, 0), (1, 2), (0, 0), (0, 0)),),
+    (((4, 6), (0, 0), (4, 6), (4, 5)),),
+    (((0, 0), (2, 3), (0, 0), (0, 0)),),
+    (((0, 0), (3, 6), (0, 2), (5, 6)),),
+    (((6, 7), (6, 7), (0, 0), (6, 7)),),
+    (((7, 8), (7, 8), (2, 4), (7, 8)), ((0, 0), (0, 0), (6, 8), (0, 0)),),
+)
 MESH = pl.DeviceIdType.MESH
 
 
@@ -18,8 +29,8 @@
     n, peers, groups, cap, width, hidden, tasks,
     counts_hbm, gate_hbm, ids_hbm, x_hbm, cot_hbm, w1_hbm, w2_hbm,
     first, second, home,
-    counts_ref, gate_ref, ids_ref, cots, tag, pay, buf, w1, w2, ret, act, pc,
-    send1, recv1, send2, recv2, send3, recv3, local_sem,
+    counts_ref, gate_ref, ids_ref, cots, tag, pay, buf, w1, w2, w1_turned, w2_turned, ret, act, pc,
+    send1, recv1, send2, recv2, send3, recv3, local_sem, ready, turn_sem,
 ):
     b = lax.axis_index("blk")
     h = lax.axis_index("dp")
@@ -27,14 +38,15 @@
     early = n - quarter
     width_part = width // peers
     hidden_part = hidden // peers
-    tile = 512
     tiles = hidden // tile
     part_tiles = hidden_part // tile
     side, place = b // half, lax.rem(b, half)
     step, spot = place // quarter, lax.rem(place, quarter)
 
-    def device_at(z, shift):
-        return z * quarter + lax.rem(spot + shift, quarter)
+    z = 2 * side + step
+
+    def device_at(floor, shift):
+        return floor * quarter + lax.rem(spot + shift, quarter)
 
     def near_target(i):
         return device_at(2 * side + step, quarter - i)
@@ -70,31 +82,93 @@
 
     barrier = pltpu.get_barrier_semaphore()
 
-    @pl.loop(1, n)
-    def _(k):
-        pl.semaphore_signal(barrier, inc=1, device_id=(lax.rem(b + k, n), h), device_id_type=MESH)
-
-    for j in range(1, peers):
-        @pl.loop(0, quarter)
-        def _(i):
-            pl.semaphore_signal(
-                barrier, inc=1, device_id=(near_target(i), lax.rem(h + j, peers)), device_id_type=MESH
-            )
+    def greet(target, j):
+        pl.semaphore_signal(barrier, inc=1, device_id=(target, lax.rem(h + j, peers)), device_id_type=MESH)
+
+    @pl.when(side == 0)
+    def _():
+        @pl.loop(1, n)
+        def _(k):
+            greet(lax.rem(b + k, n), 0)
+
+        for j in range(1, peers):
+            @pl.loop(0, quarter)
+            def _(i):
+                greet(near_target(i), j)
+
+    @pl.when(z == 2)
+    def _():
+        for j in range(peers):
+            @pl.loop(0, quarter)
+            def _(i):
+                greet(cross_target(i), j)
 
     loads = [
         pltpu.make_async_copy(source, target, local_sem.at[6 + at])
         for at, (source, target) in enumerate(
-            [(counts_hbm, counts_ref), (gate_hbm, gate_ref), (ids_hbm, ids_ref), (cot_hbm, cots)]
-            + [(x_hbm, pay.at[pl.ds(r * groups, groups), :, pl.ds(0, width)]) for r in range(n // groups)]
+            [(x_hbm, pay.at[pl.ds(r * groups, groups), :, pl.ds(0, width)]) for r in range(n // groups)]
+            + [(counts_hbm, counts_ref), (gate_hbm, gate_ref), (ids_hbm, ids_ref), (cot_hbm, cots)]
         )
     ]
-    for load in loads:
+    for load in loads[:-4]:
+        load.start()
+
+    def call(k, target, j):
+        pl.semaphore_signal(ready.at[k], inc=1, device_id=(target, lax.rem(h + j, peers)), device_id_type=MESH)
+
+    @pl.when(z == 2)
+    def _():
+        pl.semaphore_wait(barrier, half)
+
+        @pl.loop(0, half)
+        def _(i):
+            call(0, half - 1 - i, 0)
+
+    @pl.when(z == 3)
+    def _():
+        pl.semaphore_wait(barrier, half + quarter * peers)
+
+        @pl.loop(0, half)
+        def _(i):
+            call(1, i, 0)
+
+        for j in range(peers):
+            @pl.loop(0, quarter)
+            def _(i):
+                call(1, cross_target(i), j)
+
+    for load in loads[-4:]:
         load.start()
     get_w1 = pltpu.make_async_copy(w1_hbm.at[0], w1, local_sem.at[3])
-    get_w2 = pltpu.make_async_copy(w2_hbm.at[0], w2, local_sem.at[4])
+
+    def get_w2(q):
+        return pltpu.make_async_copy(w2_hbm.at[0, pl.ds(q * tile, tile)], w2.at[q % 2], turn_sem.at[q])
+
     get_w1.start()
-    get_w2.start()
-    for load in loads[:4]:
+    for q in range(2):
+        get_w2(q).start()
+
+    ahead = quarter // 2
+
+    def far_part(i, part):
+        target = far_target(i)
+        columns = pl.ds(part * width, width)
+        return pltpu.make_async_remote_copy(
+            src_ref=pay.at[target, :, columns], dst_ref=buf.at[buf_rows(0, far_slot(i)), columns],
+            send_sem=send1.at[0], recv_sem=recv1.at[far_slot(i)],
+            device_id=(target, h), device_id_type=MESH,
+        )
+
+    for load in loads[:-4]:
+        load.wait()
+
+    @pl.when(z == 2)
+    def _():
+        @pl.loop(0, ahead)
+        def _(i):
+            far_part(i, 0).start()
+
+    for load in loads[-4:]:
         load.wait()
     slots = groups * cap
     lanes = lax.broadcasted_iota(jnp.int32, (slots, slots), 1)
@@ -117,11 +191,8 @@
             gate = jnp.where(live, gate, 0.0)
             pay[r * groups + g, :, pl.ds(width, width)] = (gate * cot_rows).astype(jnp.bfloat16)
 
-    for load in loads[4:]:
-        load.wait()
     own = pltpu.make_async_copy(pay.at[b], buf.at[pl.ds(0, cap)], local_sem.at[2])
     own.start()
-    pl.semaphore_wait(barrier, n - 1 + (peers - 1) * quarter)
 
     def block_out(target, slot):
         return pltpu.make_async_remote_copy(
@@ -157,47 +228,93 @@
         for j in range(1, peers):
             forward(i, j).start()
 
-    @pl.loop(0, half)
-    def _(i):
-        block_out(far_target(i), far_slot(i)).start()
-
-    for j in range(1, peers):
+    def send_far(start, stop, stride):
+        @pl.loop(start, stop, step=stride)
+        def _(i):
+            block_out(far_target(i), far_slot(i)).start()
+
+    def send_near():
+        for j in range(1, peers):
+            @pl.loop(0, quarter)
+            def _(i):
+                across(i, j).start()
+
+        @pl.loop(1, quarter)
+        def _(i):
+            block_out(near_target(i), i).start()
+
+    def send_cross():
         @pl.loop(0, quarter)
         def _(i):
-            across(i, j).start()
-
-    @pl.loop(1, quarter)
-    def _(i):
-        block_out(near_target(i), i).start()
-
-    @pl.loop(0, quarter)
-    def _(i):
-        block_out(cross_target(i), half + i).start()
-
-    def pass_second(before, after):
-        outer = lax.rem(side + step + 1, 2)
-        start = before[0] + outer * (before[1] - before[0])
-        stop = after[0] + outer * (after[1] - after[0])
-
-        @pl.loop(half + start, half + stop)
-        def _(i):
-            pass_on(i)
+            block_out(cross_target(i), half + i).start()
+
+    @pl.when(side == 0)
+    def _():
+        pl.semaphore_wait(barrier, half - 1 + (peers - 1) * quarter)
+        send_near()
+
+        @pl.when(step == 1)
+        def _():
+            send_cross()
+
+        pl.semaphore_wait(ready.at[0], quarter)
+        send_far(0, quarter, 2)
+        pl.semaphore_wait(ready.at[1], quarter)
+        send_far(1, quarter, 2)
+        send_far(quarter, half, 1)
+
+        @pl.when(step == 0)
+        def _():
+            send_cross()
+
+    @pl.when(z == 2)
+    def _():
+        @pl.loop(0, ahead)
+        def _(i):
+            far_part(i, 1).start()
+
+        send_far(ahead, half, 1)
+        pl.semaphore_wait(ready.at[1], quarter * peers)
+        call(0, cross_target(0), 0)
+        send_near()
+        send_cross()
+
+    @pl.when(z == 3)
+    def _():
+        send_far(0, half, 1)
+        send_cross()
+        pl.semaphore_wait(ready.at[0], 1)
+        send_near()
+
+    schedule = iter(SCHEDULE)
+
+    def pick(values):
+        value = values[0]
+        for floor in range(1, 4):
+            value = jnp.where(z == floor, values[floor], value)
+        return value * quarter // 4
+
+    def poll(wanted=True):
+        if not wanted:
+            return
+        for ranges in next(schedule):
+            @pl.loop(half + pick([start for start, _ in ranges]), half + pick([stop for _, stop in ranges]))
+            def _(i):
+                pass_on(i)
+
+    get_w1.wait()
+    for q in range(tiles):
+        part = pl.ds(q * tile, tile)
+        get_w2(q).wait()
+        w2_turned[:, part] = w2[q % 2].T
+        if q + 2 < tiles:
+            get_w2(q + 2).start()
+        w1_turned[part, :] = w1[:, part].T
 
     @pl.loop(quarter, half)
     def _(i):
         pass_on(i)
 
-    points = [
-        (quarter * inner // 4, quarter * outer // 4)
-        for inner, outer in ((0, 0), (0, 4), (1, 5), (2, 5), (2, 6), (3, 6), (6, 6), (7, 7), (8, 8))
-    ]
-    met = []
-
-    def poll(wanted=True):
-        if wanted:
-            met.append(0)
-            pass_second(*points[len(met) - 1:len(met) + 1])
-
     poll()
 
     @pl.loop(1, quarter)
@@ -205,8 +322,6 @@
         block_out(b, i).wait_recv()
 
     own.wait()
-    get_w1.wait()
-    get_w2.wait()
 
     def rows_forward(start, total, hook=lambda q: None):
         rows = pl.ds(start, total)
@@ -220,8 +335,8 @@
             sig = jax.nn.sigmoid(pre)
             if q < part_tiles:
                 act[rows, pl.ds(q * tile, tile)] = (pre * sig).astype(jnp.bfloat16)
-            cot = lax.dot_general(
-                buf[rows, pl.ds(width, width)], w2[columns, :], (((1,), (1,)), ((), ())), preferred_element_type=jnp.float32
+            cot = jnp.dot(
+                buf[rows, pl.ds(width, width)], w2_turned[:, columns], preferred_element_type=jnp.float32
             )
             pc[rows, columns] = (cot * (sig * (1.0 + pre * (1.0 - sig)))).astype(jnp.bfloat16)
 
@@ -235,9 +350,7 @@
 
         for d in range(width // tile):
             columns = pl.ds(d * tile, tile)
-            grad = lax.dot_general(
-                pc[flat, :], w1[columns, :], (((1,), (1,)), ((), ())), preferred_element_type=jnp.float32
-            )
+            grad = jnp.dot(pc[flat, :], w1_turned[:, columns], preferred_element_type=jnp.float32)
             ret[rows, columns] = grad.astype(jnp.bfloat16)
             hook(d)
 
@@ -266,10 +379,16 @@
             columns = pl.ds(q * tile, tile)
             add(second, columns, act[rows, :], buf[rows, pl.ds(width + q * tile, tile)])
 
-    def release():
-        @pl.loop(quarter, half)
-        def _(i):
-            homeward(i, outer_source(i)).start()
+    def release(point):
+        @pl.when(pick([4 * (point == chosen) for chosen in RELEASE]) > 0)
+        def _():
+            @pl.loop(quarter, half)
+            def _(i):
+                homeward(i, outer_source(i)).start()
+
+    def between():
+        poll()
+        release(1)
 
     rows_forward(0, span)
     poll()
@@ -285,17 +404,11 @@
     partner_come(0)
     rows_forward(span, chunk - span, lambda q: poll(2 * (q + 1) == tiles))
     poll()
-    @pl.when(lax.rem(side + step + 1, 2) < RELEASE)
-    def _():
-        release()
-
-    grads(0, poll)
+    release(0)
+    grads(0, between)
     poll()
 
-    @pl.when(lax.rem(side + step + 1, 2) >= RELEASE)
-    def _():
-        release()
-
+    release(2)
 
     rows_forward(chunk, span)
     rows_home(1)
@@ -374,12 +487,16 @@
             pltpu.VMEM((n, cap, 2 * width), bf16),
             pltpu.VMEM((rows, 2 * width), bf16),
             pltpu.VMEM((width, hidden), bf16),
+            pltpu.VMEM((2, tile, width), bf16),
             pltpu.VMEM((hidden, width), bf16),
+            pltpu.VMEM((width, hidden), bf16),
             pltpu.VMEM((n * cap, width), bf16),
             pltpu.VMEM((rows, hidden // peers), bf16),
             pltpu.VMEM((rows, hidden), bf16),
             dma((1,)), dma((n,)), dma((peers - 1,)), dma((peers - 1, 2)), dma((1,)), dma((1,)),
             dma((10 + n // groups,)),
+            pltpu.SemaphoreType.REGULAR((2,)),
+            dma((hidden // tile,)),
         ],
         compiler_params=pltpu.CompilerParams(
             collective_id=0, has_side_effects=True, vmem_limit_bytes=VMEM_BYTES

time: 44.7 us -> 44.2 us (0.989)
  Pallas kernels: 43.9 us -> 42.8 us
    pallas_call x1, Pallas kernels: 40.4 us -> 39.3 us  [on_device(): pl.pallas_call(functools.partial(exchange_kernel, n, peers, groups, cap,...]
where the time goes in v4:
time: 44.2 us; the launch traced here: 43.6 us
  Pallas kernels  42.8 us (97%)
  between operations  0.8 us (2%)
    pallas_call x1, Pallas kernels, on_device(): pl.pallas_call(functools.partial(exchange_kernel, n, peers, groups, cap,...  39.3 us
    pallas_call x1, Pallas kernels, on_device(): pl.pallas_call(finish_kernel, out_shape=(jax.ShapeDtypeStruct((slots, wid...  3.52 us

profile of v4, /device:TPU:9, one launch (start us, length us, event | category | flops | bytes accessed | tf_op | source)
XLA Modules:
  0.0 43.6 jit_solution(15074369994165796376)
XLA Ops:
  0.6 39.3 %shard_map.94 = (f32[512,2048]{1,0:T(8,128)S(1)}, f32[1024,1024]{1,0:T(8,128)S(1)}, bf16[16,16,1024]{2,1,0:T(8,128)(2,1)S(1)}) custom-call(s32[1,8]{1,0:T(1,128)} %counts_hbm.1, f32[4,16]{1,0:T(4,128)} %gate_hbm.1, s32[1,128]{1,0:T(1,128)} %bitcast.7, bf16[8,16,1024]{2,1,0:T(8,128)(2,1)} %bitcast.5, bf16[8,16,1024]{2,1,0:T(8,128)(2,1)} %bitcast.6, ...), custom_call_target="tpu_custom_call" | custom-call | tf_op jit(solution)/shard_map/pallas_call | solution.py:472
  40.0 3.5 %shard_map.95 = (f32[128,1024]{1,0:T(8,128)}, f32[1,512,2048]{2,1,0:T(8,128)}, f32[1,1024,1024]{2,1,0:T(8,128)}) custom-call(f32[512,2048]{1,0:T(8,128)S(1)} %get-tuple-element.6.first, f32[1024,1024]{1,0:T(8,128)S(1)} %get-tuple-element.7.second, bf16[2,128,1024]{2,1,0:T(8,128)(2,1)S(1)} %bitcast.4), custom_call_target="tpu_custom_call" | custom-call | tf_op jit(solution)/shard_map/pallas_call | solution.py:513

commit v5 on v4

--- a/solution.py
+++ b/solution.py
@@ -10,7 +10,7 @@
 grad_scale = 0.0625
 VMEM_BYTES = 51 * 1024 * 1024
 PIECES = 4
-RELEASE = (2, 2, 2, 1)
+RELEASE = (2, 9, 9, 1)
 tile = 512
 SCHEDULE = (
     (((0, 4), (0, 0), (0, 0), (0, 4)),),
@@ -110,7 +110,7 @@
             + [(counts_hbm, counts_ref), (gate_hbm, gate_ref), (ids_hbm, ids_ref), (cot_hbm, cots)]
         )
     ]
-    for load in loads[:-4]:
+    for load in loads:
         load.start()
 
     def call(k, target, j):
@@ -137,8 +137,6 @@
             def _(i):
                 call(1, cross_target(i), j)
 
-    for load in loads[-4:]:
-        load.start()
     get_w1 = pltpu.make_async_copy(w1_hbm.at[0], w1, local_sem.at[3])
 
     def get_w2(q):
@@ -155,7 +153,7 @@
         columns = pl.ds(part * width, width)
         return pltpu.make_async_remote_copy(
             src_ref=pay.at[target, :, columns], dst_ref=buf.at[buf_rows(0, far_slot(i)), columns],
-            send_sem=send1.at[0], recv_sem=recv1.at[far_slot(i)],
+            send_sem=send1.at[1], recv_sem=recv1.at[far_slot(i)],
             device_id=(target, h), device_id_type=MESH,
         )
 
@@ -194,10 +192,10 @@
     own = pltpu.make_async_copy(pay.at[b], buf.at[pl.ds(0, cap)], local_sem.at[2])
     own.start()
 
-    def block_out(target, slot):
+    def block_out(target, slot, kind=0):
         return pltpu.make_async_remote_copy(
             src_ref=pay.at[target], dst_ref=buf.at[buf_rows(0, slot)],
-            send_sem=send1.at[0], recv_sem=recv1.at[slot],
+            send_sem=send1.at[kind], recv_sem=recv1.at[slot],
             device_id=(target, h), device_id_type=MESH,
         )
 
@@ -231,7 +229,7 @@
     def send_far(start, stop, stride):
         @pl.loop(start, stop, step=stride)
         def _(i):
-            block_out(far_target(i), far_slot(i)).start()
+            block_out(far_target(i), far_slot(i), 1).start()
 
     def send_near():
         for j in range(1, peers):
@@ -379,12 +377,23 @@
             columns = pl.ds(q * tile, tile)
             add(second, columns, act[rows, :], buf[rows, pl.ds(width + q * tile, tile)])
 
+    outer = lax.rem(side + step, 2) == 0
+
+    def far_sent():
+        sent = pay.at[pl.ds(0, half)]
+        pltpu.make_async_copy(sent, sent, send1.at[1]).wait()
+
+    kept = half - (1 - side) * (quarter // 4)
+
+    def send_outer(start, stop):
+        @pl.loop(start, stop)
+        def _(i):
+            homeward(i, outer_source(i)).start()
+
     def release(point):
         @pl.when(pick([4 * (point == chosen) for chosen in RELEASE]) > 0)
         def _():
-            @pl.loop(quarter, half)
-            def _(i):
-                homeward(i, outer_source(i)).start()
+            send_outer(quarter, kept)
 
     def between():
         poll()
@@ -406,6 +415,12 @@
     poll()
     release(0)
     grads(0, between)
+
+    @pl.when(jnp.logical_not(outer))
+    def _():
+        far_sent()
+        send_outer(quarter, kept)
+
     poll()
 
     release(2)
@@ -417,6 +432,8 @@
     def _(i):
         homeward(i, inner_source(i)).start()
 
+    send_outer(kept, half)
+
     @pl.loop(half, early)
     def _(i):
         homeward(i, cross_source(i)).start()
@@ -428,8 +445,13 @@
 
     own_home.wait()
 
-    sent = pay.at[pl.ds(0, n - 1)]
+    sent = pay.at[pl.ds(0, half - 1)]
     pltpu.make_async_copy(sent, sent, send1.at[0]).wait()
+
+    @pl.when(outer)
+    def _():
+        far_sent()
+
     for j in range(1, peers):
         whole = buf.at[pl.ds(0, 2 * span)]
         pltpu.make_async_copy(whole, whole, send2.at[j - 1]).wait()
@@ -493,7 +515,7 @@
             pltpu.VMEM((n * cap, width), bf16),
             pltpu.VMEM((rows, hidden // peers), bf16),
             pltpu.VMEM((rows, hidden), bf16),
-            dma((1,)), dma((n,)), dma((peers - 1,)), dma((peers - 1, 2)), dma((1,)), dma((1,)),
+            dma((2,)), dma((n,)), dma((peers - 1,)), dma((peers - 1, 2)), dma((1,)), dma((1,)),
             dma((10 + n // groups,)),
             pltpu.SemaphoreType.REGULAR((2,)),
             dma((hidden // tile,)),

time: 44.2 us -> 43.8 us (level)
  Pallas kernels: 42.8 us -> 42.2 us
    pallas_call x1, Pallas kernels: 39.3 us -> 38.6 us  [on_device(): pl.pallas_call(functools.partial(exchange_kernel, n, peers, groups, cap,...]
where the time goes in v5:
time: 43.8 us; the launch traced here: 43 us
  Pallas kernels  42.2 us (96%)
  between operations  0.8 us (2%)
    pallas_call x1, Pallas kernels, on_device(): pl.pallas_call(functools.partial(exchange_kernel, n, peers, groups, cap,...  38.6 us
    pallas_call x1, Pallas kernels, on_device(): pl.pallas_call(finish_kernel, out_shape=(jax.ShapeDtypeStruct((slots, wid...  3.52 us

profile of v5, /device:TPU:9, one launch (start us, length us, event | category | flops | bytes accessed | tf_op | source)
XLA Modules:
  0.0 43.0 jit_solution(16681784305055947925)
XLA Ops:
  0.6 38.6 %shard_map.94 = (f32[512,2048]{1,0:T(8,128)S(1)}, f32[1024,1024]{1,0:T(8,128)S(1)}, bf16[16,16,1024]{2,1,0:T(8,128)(2,1)S(1)}) custom-call(s32[1,8]{1,0:T(1,128)} %counts_hbm.1, f32[4,16]{1,0:T(4,128)} %gate_hbm.1, s32[1,128]{1,0:T(1,128)} %bitcast.7, bf16[8,16,1024]{2,1,0:T(8,128)(2,1)} %bitcast.5, bf16[8,16,1024]{2,1,0:T(8,128)(2,1)} %bitcast.6, ...), custom_call_target="tpu_custom_call" | custom-call | tf_op jit(solution)/shard_map/pallas_call | solution.py:494
  39.3 3.5 %shard_map.95 = (f32[128,1024]{1,0:T(8,128)}, f32[1,512,2048]{2,1,0:T(8,128)}, f32[1,1024,1024]{2,1,0:T(8,128)}) custom-call(f32[512,2048]{1,0:T(8,128)S(1)} %get-tuple-element.6.first, f32[1024,1024]{1,0:T(8,128)S(1)} %get-tuple-element.7.second, bf16[2,128,1024]{2,1,0:T(8,128)(2,1)S(1)} %bitcast.4), custom_call_target="tpu_custom_call" | custom-call | tf_op jit(solution)/shard_map/pallas_call | solution.py:535

commit v6 on v5

--- a/solution.py
+++ b/solution.py
@@ -383,17 +383,18 @@
         sent = pay.at[pl.ds(0, half)]
         pltpu.make_async_copy(sent, sent, send1.at[1]).wait()
 
-    kept = half - (1 - side) * (quarter // 4)
-
-    def send_outer(start, stop):
+    kept = quarter - (1 - side) * (quarter // 4)
+
+    def send_back(base, source, start, stop):
         @pl.loop(start, stop)
-        def _(i):
-            homeward(i, outer_source(i)).start()
+        def _(t):
+            i = base + lax.rem(t - spot + quarter, quarter)
+            homeward(i, source(i)).start()
 
     def release(point):
         @pl.when(pick([4 * (point == chosen) for chosen in RELEASE]) > 0)
         def _():
-            send_outer(quarter, kept)
+            send_back(quarter, outer_source, 0, kept)
 
     def between():
         poll()
@@ -419,7 +420,7 @@
     @pl.when(jnp.logical_not(outer))
     def _():
         far_sent()
-        send_outer(quarter, kept)
+        send_back(quarter, outer_source, 0, kept)
 
     poll()
 
@@ -428,15 +429,11 @@
     rows_forward(chunk, span)
     rows_home(1)
 
-    @pl.loop(early, n)
-    def _(i):
-        homeward(i, inner_source(i)).start()
-
-    send_outer(kept, half)
-
-    @pl.loop(half, early)
-    def _(i):
-        homeward(i, cross_source(i)).start()
+    send_back(early, inner_source, 0, quarter)
+
+    send_back(quarter, outer_source, kept, quarter)
+
+    send_back(half, cross_source, 0, quarter)
 
     partner_come(1)
     rows_forward(chunk + span, chunk - span)

time: 43.8 us -> 42.9 us (0.979)
  Pallas kernels: 42.2 us -> 41.5 us
    pallas_call x1, Pallas kernels: 38.6 us -> 37.9 us  [on_device(): pl.pallas_call(functools.partial(exchange_kernel, n, peers, groups, cap,...]
where the time goes in v6:
time: 42.9 us; the launch traced here: 42.3 us
  Pallas kernels  41.5 us (97%)
  between operations  0.8 us (2%)
    pallas_call x1, Pallas kernels, on_device(): pl.pallas_call(functools.partial(exchange_kernel, n, peers, groups, cap,...  37.9 us
    pallas_call x1, Pallas kernels, on_device(): pl.pallas_call(finish_kernel, out_shape=(jax.ShapeDtypeStruct((slots, wid...  3.52 us

profile of v6, /device:TPU:9, one launch (start us, length us, event | category | flops | bytes accessed | tf_op | source)
XLA Modules:
  0.0 42.3 jit_solution(13776309293145693837)
XLA Ops:
  0.6 37.9 %shard_map.94 = (f32[512,2048]{1,0:T(8,128)S(1)}, f32[1024,1024]{1,0:T(8,128)S(1)}, bf16[16,16,1024]{2,1,0:T(8,128)(2,1)S(1)}) custom-call(s32[1,8]{1,0:T(1,128)} %counts_hbm.1, f32[4,16]{1,0:T(4,128)} %gate_hbm.1, s32[1,128]{1,0:T(1,128)} %bitcast.7, bf16[8,16,1024]{2,1,0:T(8,128)(2,1)} %bitcast.5, bf16[8,16,1024]{2,1,0:T(8,128)(2,1)} %bitcast.6, ...), custom_call_target="tpu_custom_call" | custom-call | tf_op jit(solution)/shard_map/pallas_call | solution.py:491
  38.6 3.5 %shard_map.95 = (f32[128,1024]{1,0:T(8,128)}, f32[1,512,2048]{2,1,0:T(8,128)}, f32[1,1024,1024]{2,1,0:T(8,128)}) custom-call(f32[512,2048]{1,0:T(8,128)S(1)} %get-tuple-element.6.first, f32[1024,1024]{1,0:T(8,128)S(1)} %get-tuple-element.7.second, bf16[2,128,1024]{2,1,0:T(8,128)(2,1)S(1)} %bitcast.4), custom_call_target="tpu_custom_call" | custom-call | tf_op jit(solution)/shard_map/pallas_call | solution.py:532

commit v7 on v6

--- a/solution.py
+++ b/solution.py
@@ -383,11 +383,13 @@
         sent = pay.at[pl.ds(0, half)]
         pltpu.make_async_copy(sent, sent, send1.at[1]).wait()
 
-    kept = quarter - (1 - side) * (quarter // 4)
+    kept = quarter - (1 - side) * step * (quarter // 4)
 
     def send_back(base, source, start, stop):
         @pl.loop(start, stop)
-        def _(t):
+        def _(at):
+            turned_back = at // (quarter // 2) * lax.rem(spot, 2)
+            t = at + turned_back * (quarter + quarter // 2 - 1 - 2 * at)
             i = base + lax.rem(t - spot + quarter, quarter)
             homeward(i, source(i)).start()
 

time: 42.9 us -> 42.9 us (level)
  no operation moved by 1% of the time
where the time goes in v7:
time: 42.9 us; the launch traced here: 42.3 us
  Pallas kernels  41.5 us (97%)
  between operations  0.8 us (2%)
    pallas_call x1, Pallas kernels, on_device(): pl.pallas_call(functools.partial(exchange_kernel, n, peers, groups, cap,...  37.9 us
    pallas_call x1, Pallas kernels, on_device(): pl.pallas_call(finish_kernel, out_shape=(jax.ShapeDtypeStruct((slots, wid...  3.52 us

profile of v7, /device:TPU:9, one launch (start us, length us, event | category | flops | bytes accessed | tf_op | source)
XLA Modules:
  0.0 42.3 jit_solution(15641460113232265501)
XLA Ops:
  0.6 37.9 %shard_map.94 = (f32[512,2048]{1,0:T(8,128)S(1)}, f32[1024,1024]{1,0:T(8,128)S(1)}, bf16[16,16,1024]{2,1,0:T(8,128)(2,1)S(1)}) custom-call(s32[1,8]{1,0:T(1,128)} %counts_hbm.1, f32[4,16]{1,0:T(4,128)} %gate_hbm.1, s32[1,128]{1,0:T(1,128)} %bitcast.7, bf16[8,16,1024]{2,1,0:T(8,128)(2,1)} %bitcast.5, bf16[8,16,1024]{2,1,0:T(8,128)(2,1)} %bitcast.6, ...), custom_call_target="tpu_custom_call" | custom-call | tf_op jit(solution)/shard_map/pallas_call | solution.py:493
  38.6 3.5 %shard_map.95 = (f32[128,1024]{1,0:T(8,128)}, f32[1,512,2048]{2,1,0:T(8,128)}, f32[1,1024,1024]{2,1,0:T(8,128)}) custom-call(f32[512,2048]{1,0:T(8,128)S(1)} %get-tuple-element.6.first, f32[1024,1024]{1,0:T(8,128)S(1)} %get-tuple-element.7.second, bf16[2,128,1024]{2,1,0:T(8,128)(2,1)S(1)} %bitcast.4), custom_call_target="tpu_custom_call" | custom-call | tf_op jit(solution)/shard_map/pallas_call | solution.py:534
